TPU v7x, 32 devices: a whole 2x2x4 slice. The times are simulated.
32 devices in a mesh: scen: 8 (over z, x), blk: 4 (over y, core).
Axes of the slice: x: 2, y: 2, z: 4, core: 2. Of those that a mesh axis runs over, the one named last changes fastest.
Arguments:
- cons_matrix: bfloat16 [2048, 4096], P(None, 'blk'), may hold values from -0.09375 to 0.09375
- row_scale: float32 [512, 2048], P('scen'), may hold values from 0.5 to 2
- rhs: float32 [512, 2048], P('scen'), may hold values from -6 to 6
- cons_mult: float32 [512, 2048], P('scen'), may hold values from -3 to 3
- cost: float32 [512, 4096], P('scen', 'blk'), may hold values from -6 to 6
- ph_mult: float32 [512, 4096], P('scen', 'blk'), may hold values from -3 to 3
- start: float32 [512, 4096], P('scen', 'blk'), may hold values from -3 to 3
- consensus: float32 [4096], P('blk'), may hold values from -3 to 3
- upper: float32 [4096], P('blk'), may hold values from 0.3 to 1.5
- prob: float32 [512], P('scen'), may hold values from 1 to 30, as said below
Outputs:
- solutions: float32 [512, 4096], P('scen', 'blk')
- mult_new: float32 [512, 2048], P('scen', 'blk')
- z_new: float32 [4096], P('blk')
- w_new: float32 [512, 4096], P('scen', 'blk')
- primal_res: float32 [], replicated
- dual_res: float32 [], replicated
Inputs may be any that keep to these rules, and one draw needn't show every extreme that they name: prob is positive.
All inputs are finite; a program needn't handle non-finite values.
Results may differ from a plain program's by a relative error of at most 0.0017.
Values may be sent and summed in bfloat16 or wider, within the bound.
A program may use at most 64 MiB of HBM per device.

v0:
```python
import jax
import jax.numpy as jnp
from jax import lax
from jax.sharding import PartitionSpec as P

NV = 4096
ITERS = 8
penalty = 1.0
aug_weight = 1.0
step_size = 0.05
eps = 1e-06


def per_device(
    cons_matrix, row_scale, rhs, cons_mult, cost, ph_mult, start, consensus, upper, prob
):
    n_blk = lax.axis_size("blk")
    n_scen = lax.axis_size("scen")
    share_rows = cons_matrix.shape[0] // n_blk
    first_row = lax.axis_index("blk") * share_rows
    own_scale = lax.dynamic_slice_in_dim(row_scale, first_row, share_rows, 1)
    own_rhs = lax.dynamic_slice_in_dim(rhs, first_row, share_rows, 1)
    own_mult = lax.dynamic_slice_in_dim(cons_mult, first_row, share_rows, 1)
    contract = (((1,), (1,)), ((), ()))
    x_now = start
    low_box = -upper[None, :]
    high_box = upper[None, :]
    for step in range(ITERS):
        partial_value = lax.dot_general(
            x_now.astype(jnp.bfloat16), cons_matrix, contract, preferred_element_type=jnp.float32
        )
        prod_share = lax.psum_scatter(partial_value, "blk", scatter_dimension=1, tiled=True)
        weighted_share = (
            own_scale * (own_mult + aug_weight * (own_scale * prod_share - own_rhs))
        ).astype(jnp.bfloat16)
        back = jnp.dot(
            lax.all_gather(weighted_share, "blk", axis=1, tiled=True),
            cons_matrix,
            preferred_element_type=jnp.float32,
        )
        grad = cost + ph_mult + penalty * (x_now - consensus[None, :]) + back
        x_now = jnp.clip(x_now - step_size * grad, low_box, high_box)
    partial_end = lax.dot_general(
        x_now.astype(jnp.bfloat16), cons_matrix, contract, preferred_element_type=jnp.float32
    )
    prod_end = lax.psum_scatter(partial_end, "blk", scatter_dimension=1, tiled=True)
    mult_new = own_mult + aug_weight * (own_scale * prod_end - own_rhs)
    weighted_x = prob[:, None] * x_now
    local_sum = jnp.sum(weighted_x, axis=0)
    local_total = jnp.sum(prob)
    sums, total = lax.psum((local_sum, local_total), "scen")
    z_new = sums / total
    primal_local = jnp.sum(prob[:, None] * (x_now - z_new[None, :]) ** 2)
    dual_local = jnp.sum((z_new - consensus) ** 2) * (1.0 / n_scen)
    primal_sum, dual_sum = lax.psum((primal_local, dual_local), ("scen", "blk"))
    w_new = ph_mult + penalty * (x_now - z_new[None, :])
    primal_res = jnp.sqrt(primal_sum / (total * NV) + eps)
    dual_res = penalty * jnp.sqrt(dual_sum / NV + eps)
    return (x_now, mult_new, z_new, w_new, primal_res, dual_res)


def solution(mesh):
    in_specs = (
        P(None, "blk"),
        P("scen", None),
        P("scen", None),
        P("scen", None),
        P("scen", "blk"),
        P("scen", "blk"),
        P("scen", "blk"),
        P("blk"),
        P("blk"),
        P("scen"),
    )
    out_specs = (P("scen", "blk"), P("scen", "blk"), P("blk"), P("scen", "blk"), P(), P())
    return jax.shard_map(
        per_device, mesh=mesh, in_specs=in_specs, out_specs=out_specs, check_vma=False
    )
```

profile of v0, /device:TPU:12, one launch (start us, length us, event | category | flops | bytes accessed | tf_op | source)
XLA Modules:
  0.0 364.3 jit_solution(18422176172987149110)
XLA Ops:
  7.3 4.6 %fusion.48 = f32[64,2048]{1,0:T(8,128)} fusion(bf16[2048,1024]{1,0:T(8,128)(2,1)} %param.10, f32[64,1024]{1,0:T(8,128)} %param.16), kind=kOutput, calls=%fused_computation.68 | convolution fusion | flops 268500992 | bytes 4980736 | tf_op jit(solution)/shard_map/dot_general | solution.py:29
  12.1 21.8 %reduce-scatter.10.cloned.1.call-done = f32[64,512]{1,0:T(8,128)} async-done(((f32[64,2048]{1,0:T(8,128)}), f32[64,512]{1,0:T(8,128)}) %reduce-scatter.10.cloned.1.call-update) | async-done | bytes 131088 | tf_op jit(solution)/shard_map/reduce_scatter | solution.py:32
  35.0 5.9 %all_gather.24 = bf16[64,2048]{1,0:T(8,128)(2,1)S(1)} all-gather(bf16[64,512]{1,0:T(8,128)(2,1)S(1)} %multiply_convert_fusion.7), channel_id=1, replica_groups=mesh['scen'=8,'blk'=4] {'blk'}, dimensions={1}, use_global_device_ids=true | all-gather | bytes 327680 | tf_op jit(solution)/shard_map/all_gather | solution.py:37
  40.9 3.1 fusion.17
  46.3 21.8 %reduce-scatter.12.cloned.1.call-done = f32[64,512]{1,0:T(8,128)} async-done(((f32[64,2048]{1,0:T(8,128)}), f32[64,512]{1,0:T(8,128)}) %reduce-scatter.12.cloned.1.call-update) | async-done | bytes 131088 | tf_op jit(solution)/shard_map/reduce_scatter | solution.py:32
  69.2 5.9 %all_gather.25 = bf16[64,2048]{1,0:T(8,128)(2,1)S(1)} all-gather(bf16[64,512]{1,0:T(8,128)(2,1)S(1)} %multiply_convert_fusion.6), channel_id=1, replica_groups=mesh['scen'=8,'blk'=4] {'blk'}, dimensions={1}, use_global_device_ids=true | all-gather | bytes 327680 | tf_op jit(solution)/shard_map/all_gather | solution.py:37
  75.1 3.1 fusion.19
  80.5 21.8 %reduce-scatter.14.cloned.1.call-done = f32[64,512]{1,0:T(8,128)} async-done(((f32[64,2048]{1,0:T(8,128)}), f32[64,512]{1,0:T(8,128)}) %reduce-scatter.14.cloned.1.call-update) | async-done | bytes 131088 | tf_op jit(solution)/shard_map/reduce_scatter | solution.py:32
  103.3 5.9 %all_gather.26 = bf16[64,2048]{1,0:T(8,128)(2,1)S(1)} all-gather(bf16[64,512]{1,0:T(8,128)(2,1)S(1)} %multiply_convert_fusion.5), channel_id=1, replica_groups=mesh['scen'=8,'blk'=4] {'blk'}, dimensions={1}, use_global_device_ids=true | all-gather | bytes 327680 | tf_op jit(solution)/shard_map/all_gather | solution.py:37
  114.6 21.8 %reduce-scatter.16.cloned.1.call-done = f32[64,512]{1,0:T(8,128)} async-done(((f32[64,2048]{1,0:T(8,128)}), f32[64,512]{1,0:T(8,128)}) %reduce-scatter.16.cloned.1.call-update) | async-done | bytes 131088 | tf_op jit(solution)/shard_map/reduce_scatter | solution.py:32
  137.5 5.9 %all_gather.27 = bf16[64,2048]{1,0:T(8,128)(2,1)S(1)} all-gather(bf16[64,512]{1,0:T(8,128)(2,1)S(1)} %multiply_convert_fusion.4), channel_id=1, replica_groups=mesh['scen'=8,'blk'=4] {'blk'}, dimensions={1}, use_global_device_ids=true | all-gather | bytes 327680 | tf_op jit(solution)/shard_map/all_gather | solution.py:37
  143.4 3.1 fusion.23
  148.8 21.8 %reduce-scatter.18.cloned.1.call-done = f32[64,512]{1,0:T(8,128)} async-done(((f32[64,2048]{1,0:T(8,128)}), f32[64,512]{1,0:T(8,128)}) %reduce-scatter.18.cloned.1.call-update) | async-done | bytes 131088 | tf_op jit(solution)/shard_map/reduce_scatter | solution.py:32
  171.6 5.9 %all_gather.28 = bf16[64,2048]{1,0:T(8,128)(2,1)S(1)} all-gather(bf16[64,512]{1,0:T(8,128)(2,1)S(1)} %multiply_convert_fusion.3), channel_id=1, replica_groups=mesh['scen'=8,'blk'=4] {'blk'}, dimensions={1}, use_global_device_ids=true | all-gather | bytes 327680 | tf_op jit(solution)/shard_map/all_gather | solution.py:37
  183.1 21.6 %reduce-scatter.20.cloned.1.call-done = f32[64,512]{1,0:T(8,128)} async-done(((f32[64,2048]{1,0:T(8,128)}), f32[64,512]{1,0:T(8,128)}) %reduce-scatter.20.cloned.1.call-update) | async-done | bytes 131088 | tf_op jit(solution)/shard_map/reduce_scatter | solution.py:32
  205.8 5.9 %all_gather.29 = bf16[64,2048]{1,0:T(8,128)(2,1)S(1)} all-gather(bf16[64,512]{1,0:T(8,128)(2,1)S(1)} %multiply_convert_fusion.2), channel_id=1, replica_groups=mesh['scen'=8,'blk'=4] {'blk'}, dimensions={1}, use_global_device_ids=true | all-gather | bytes 327680 | tf_op jit(solution)/shard_map/all_gather | solution.py:37
  211.7 3.1 fusion.27
  217.1 21.8 %reduce-scatter.22.cloned.1.call-done = f32[64,512]{1,0:T(8,128)} async-done(((f32[64,2048]{1,0:T(8,128)}), f32[64,512]{1,0:T(8,128)}) %reduce-scatter.22.cloned.1.call-update) | async-done | bytes 131088 | tf_op jit(solution)/shard_map/reduce_scatter | solution.py:32
  240.0 5.9 %all_gather.30 = bf16[64,2048]{1,0:T(8,128)(2,1)S(1)} all-gather(bf16[64,512]{1,0:T(8,128)(2,1)S(1)} %multiply_convert_fusion.1), channel_id=1, replica_groups=mesh['scen'=8,'blk'=4] {'blk'}, dimensions={1}, use_global_device_ids=true | all-gather | bytes 327680 | tf_op jit(solution)/shard_map/all_gather | solution.py:37
  251.3 21.8 %reduce-scatter.24.cloned.1.call-done = f32[64,512]{1,0:T(8,128)} async-done(((f32[64,2048]{1,0:T(8,128)}), f32[64,512]{1,0:T(8,128)}) %reduce-scatter.24.cloned.1.call-update) | async-done | bytes 131088 | tf_op jit(solution)/shard_map/reduce_scatter | solution.py:32
  274.1 5.9 %all_gather.31 = bf16[64,2048]{1,0:T(8,128)(2,1)S(1)} all-gather(bf16[64,512]{1,0:T(8,128)(2,1)S(1)} %multiply_convert_fusion), channel_id=1, replica_groups=mesh['scen'=8,'blk'=4] {'blk'}, dimensions={1}, use_global_device_ids=true | all-gather | bytes 327680 | tf_op jit(solution)/shard_map/all_gather | solution.py:37
  280.0 3.1 multiply_reduce_fusion.1
  286.0 19.5 %all-reduce.1 = (f32[1024]{0:T(1024)S(1)}, f32[]{:T(128)}) all-reduce(f32[1024]{0:T(1024)S(1)} %get-tuple-element.14, f32[]{:T(128)} %reduce_sum.37), channel_id=1, replica_groups=mesh['scen'=8,'blk'=4] {'scen'}, use_global_device_ids=true, to_apply=%region_10.11 | all-reduce | flops 1025 | bytes 8200 | tf_op jit(solution)/shard_map/psum | solution.py:51
  308.7 43.1 %all-reduce = (f32[]{:T(128)}, f32[]{:T(128)}) all-reduce(f32[]{:T(128)} %get-tuple-element.12, f32[]{:T(128)S(6)} %mul.128), channel_id=1, replica_groups=mesh['scen'=8,'blk'=4] {'scen','blk'}, use_global_device_ids=true, to_apply=%region_14.15 | all-reduce | flops 2 | bytes 16 | tf_op jit(solution)/shard_map/psum | solution.py:55
  (82 shorter events, 41.2 us)
Async XLA Ops:
  7.2 33.8 %copy-start.12 = (f32[64,1024]{1,0:T(8,128)S(1)}, f32[64,1024]{1,0:T(8,128)}, u32[]{:S(2)}) copy-start(f32[64,1024]{1,0:T(8,128)} %param.16) | copy-start | bytes 786436
  7.2 26.7 %copy-start.8 = (f32[64,2048]{1,0:T(8,128)S(1)}, f32[64,2048]{1,0:T(8,128)}, u32[]{:S(2)}) copy-start(f32[64,2048]{1,0:T(8,128)} %param.12) | copy-start | bytes 1572868
  7.2 26.7 %copy-start.9 = (f32[64,2048]{1,0:T(8,128)S(1)}, f32[64,2048]{1,0:T(8,128)}, u32[]{:S(2)}) copy-start(f32[64,2048]{1,0:T(8,128)} %param.13) | copy-start | bytes 1572868
  7.2 26.7 %copy-start.10 = (f32[64,2048]{1,0:T(8,128)S(1)}, f32[64,2048]{1,0:T(8,128)}, u32[]{:S(2)}) copy-start(f32[64,2048]{1,0:T(8,128)} %param.11) | copy-start | bytes 1572868
  7.2 33.7 %copy-start.15 = (f32[1024]{0:T(1024)S(1)}, f32[1024]{0:T(1024)}, u32[]{:S(2)}) copy-start(f32[1024]{0:T(1024)} %param.17) | copy-start | bytes 12292
  7.2 26.6 %reduce-scatter.10.cloned.1.call-start = ((), (), s32[]{:S(2)}) async-start(), calls=%async_computation.9 | async-start | bytes 655360 | tf_op jit(solution)/shard_map/reduce_scatter | solution.py:32
  11.9 56.2 %reduce-scatter.12.cloned.1.call-start = ((), (), s32[]{:S(2)}) async-start(), calls=%async_computation.10 | async-start | bytes 655360 | tf_op jit(solution)/shard_map/reduce_scatter | solution.py:32
  33.9 10.1 %copy-start = (bf16[2048,1024]{1,0:T(8,128)(2,1)S(1)}, bf16[2048,1024]{1,0:T(8,128)(2,1)}, u32[]{:S(2)}) copy-start(bf16[2048,1024]{1,0:T(8,128)(2,1)} %param.10) | copy-start | bytes 12582916
  46.3 56.0 %reduce-scatter.14.cloned.1.call-start = ((), (), s32[]{:S(2)}) async-start(), calls=%async_computation.11 | async-start | bytes 655360 | tf_op jit(solution)/shard_map/reduce_scatter | solution.py:32
  68.1 10.1 %copy-start.1 = (bf16[2048,1024]{1,0:T(8,128)(2,1)S(1)}, bf16[2048,1024]{1,0:T(8,128)(2,1)}, u32[]{:S(2)}) copy-start(bf16[2048,1024]{1,0:T(8,128)(2,1)} %param.10) | copy-start | bytes 12582916
  80.4 56.0 %reduce-scatter.16.cloned.1.call-start = ((), (), s32[]{:S(2)}) async-start(), calls=%async_computation.12 | async-start | bytes 655360 | tf_op jit(solution)/shard_map/reduce_scatter | solution.py:32
  102.2 10.1 %copy-start.2 = (bf16[2048,1024]{1,0:T(8,128)(2,1)S(1)}, bf16[2048,1024]{1,0:T(8,128)(2,1)}, u32[]{:S(2)}) copy-start(bf16[2048,1024]{1,0:T(8,128)(2,1)} %param.10) | copy-start | bytes 12582916
  114.6 56.0 %reduce-scatter.18.cloned.1.call-start = ((), (), s32[]{:S(2)}) async-start(), calls=%async_computation.13 | async-start | bytes 655360 | tf_op jit(solution)/shard_map/reduce_scatter | solution.py:32
  136.4 10.1 %copy-start.3 = (bf16[2048,1024]{1,0:T(8,128)(2,1)S(1)}, bf16[2048,1024]{1,0:T(8,128)(2,1)}, u32[]{:S(2)}) copy-start(bf16[2048,1024]{1,0:T(8,128)(2,1)} %param.10) | copy-start | bytes 12582916
  148.7 56.0 %reduce-scatter.20.cloned.1.call-start = ((), (), s32[]{:S(2)}) async-start(), calls=%async_computation.14 | async-start | bytes 655360 | tf_op jit(solution)/shard_map/reduce_scatter | solution.py:32
  182.9 56.0 %reduce-scatter.22.cloned.1.call-start = ((), (), s32[]{:S(2)}) async-start(), calls=%async_computation.15 | async-start | bytes 655360 | tf_op jit(solution)/shard_map/reduce_scatter | solution.py:32
  204.7 10.1 %copy-start.5 = (bf16[2048,1024]{1,0:T(8,128)(2,1)S(1)}, bf16[2048,1024]{1,0:T(8,128)(2,1)}, u32[]{:S(2)}) copy-start(bf16[2048,1024]{1,0:T(8,128)(2,1)} %param.10) | copy-start | bytes 12582916
  217.1 56.0 %reduce-scatter.24.cloned.1.call-start = ((), (), s32[]{:S(2)}) async-start(), calls=%async_computation.16 | async-start | bytes 655360 | tf_op jit(solution)/shard_map/reduce_scatter | solution.py:32
  238.9 10.1 %copy-start.6 = (bf16[2048,1024]{1,0:T(8,128)(2,1)S(1)}, bf16[2048,1024]{1,0:T(8,128)(2,1)}, u32[]{:S(2)}) copy-start(bf16[2048,1024]{1,0:T(8,128)(2,1)} %param.10) | copy-start | bytes 12582916
  249.0 31.1 %copy-start.18 = (f32[64]{0:T(128)S(1)}, f32[64]{0:T(128)}, u32[]{:S(2)}) copy-start(f32[64]{0:T(128)} %param.19) | copy-start | bytes 772
  251.2 102.7 %reduce-scatter.26.cloned.1.call-start = ((), (), s32[]{:S(2)}) async-start(), calls=%async_computation.17 | async-start | bytes 655360 | tf_op jit(solution)/shard_map/reduce_scatter | solution.py:46
  273.0 10.2 %copy-start.7 = (bf16[2048,1024]{1,0:T(8,128)(2,1)S(1)}, bf16[2048,1024]{1,0:T(8,128)(2,1)}, u32[]{:S(2)}) copy-start(bf16[2048,1024]{1,0:T(8,128)(2,1)} %param.10) | copy-start | bytes 12582916
  283.2 72.3 %copy-start.11 = (f32[64,1024]{1,0:T(8,128)}, f32[64,1024]{1,0:T(8,128)S(1)}, u32[]{:S(2)}) copy-start(f32[64,1024]{1,0:T(8,128)S(1)} %get-tuple-element.15) | copy-start | bytes 786436
  306.7 48.7 %copy-start.17 = (f32[1024]{0:T(1024)}, f32[1024]{0:T(1024)S(1)}, u32[]{:S(2)}) copy-start(f32[1024]{0:T(1024)S(1)} %get-tuple-element.11) | copy-start | bytes 12292
  (4 other events, 24.5 us)
Sparse Core Ops, SparseCore 0:
  12.0 21.8 reduce-scatter.9
  46.4 21.6 reduce-scatter.11
  80.5 21.6 reduce-scatter.13
  114.7 21.6 reduce-scatter.15
  148.9 21.6 reduce-scatter.17
  183.0 21.6 reduce-scatter.19
  217.2 21.6 reduce-scatter.21
  251.3 21.6 reduce-scatter.23
  285.5 21.6 reduce-scatter.25
where the time goes:
time: 365 us; the launch traced here: 364 us
  waiting for transfers between devices  174 us (48%)
  blocking collectives  110 us (30%)
  matrix products  46.9 us (13%)
  between operations  19.1 us (5%)
  other arithmetic  13.6 us (4%)
    reduce_scatter x8, waiting for transfers between devices, per_device(): lax.psum_scatter(partial_value, 'blk', scatter_dimension=1, tiled=True)  174 us
    all_gather x8, blocking collectives, per_device(): lax.all_gather(weighted_share, 'blk', axis=1, tiled=True)  47.3 us
    psum x1, blocking collectives, per_device(): primal_sum, dual_sum = lax.psum((primal_local, dual_local), ('scen', 'blk'))  43.1 us
    dot_general x8, matrix products, per_device(): jnp.dot(lax.all_gather(weighted_share, 'blk', axis=1, tiled=True), cons_m...  24.7 us
    dot_general x9, matrix products, per_device(): lax.dot_general(x_now.astype(jnp.bfloat16), cons_matrix, contract, prefer...  22.2 us
    psum x1, blocking collectives, per_device(): sums, total = lax.psum((local_sum, local_total), 'scen')  19.5 us
    convert_element_type x8, other arithmetic, per_device(): weighted_share = (own_scale * (own_mult + aug_weight * (own_scale * prod_...  8.73 us
  transfers between devices with their start and end apart: 9, of which 8 were waited for; matrix products, arithmetic and copies ran while one was open for 1% of the time, Pallas kernels for 0%

commit v1 on v0

--- a/solution.py
+++ b/solution.py
@@ -52,7 +52,9 @@
     z_new = sums / total
     primal_local = jnp.sum(prob[:, None] * (x_now - z_new[None, :]) ** 2)
     dual_local = jnp.sum((z_new - consensus) ** 2) * (1.0 / n_scen)
-    primal_sum, dual_sum = lax.psum((primal_local, dual_local), ("scen", "blk"))
+    primal_sum, dual_sum = lax.psum(
+        lax.psum((primal_local, dual_local), axis_name="blk"), axis_name="scen"
+    )
     w_new = ph_mult + penalty * (x_now - z_new[None, :])
     primal_res = jnp.sqrt(primal_sum / (total * NV) + eps)
     dual_res = penalty * jnp.sqrt(dual_sum / NV + eps)

time: 365 us -> 351 us (0.962); the launches traced: 364 us -> 345 us
  blocking collectives: 110 us -> 90.8 us
    psum x1 -> x2, blocking collectives: 43.1 us -> 24 us  [the longest x1 17.7 us: per_device(): lax.psum(lax.psum((primal_local, dual_local), axis_name='blk'), axis_name...]
where the time goes in v1:
time: 351 us; the launch traced here: 345 us
  waiting for transfers between devices  174 us (50%)
  blocking collectives  90.8 us (26%)
  matrix products  46.9 us (13%)
  between operations  19.1 us (5%)
  other arithmetic  13.6 us (4%)
    reduce_scatter x8, waiting for transfers between devices, per_device(): lax.psum_scatter(partial_value, 'blk', scatter_dimension=1, tiled=True)  174 us
    all_gather x8, blocking collectives, per_device(): lax.all_gather(weighted_share, 'blk', axis=1, tiled=True)  47.3 us
    dot_general x8, matrix products, per_device(): jnp.dot(lax.all_gather(weighted_share, 'blk', axis=1, tiled=True), cons_m...  24.7 us
    dot_general x9, matrix products, per_device(): lax.dot_general(x_now.astype(jnp.bfloat16), cons_matrix, contract, prefer...  22.2 us
    psum x1, blocking collectives, per_device(): sums, total = lax.psum((local_sum, local_total), 'scen')  19.5 us
    psum x1, blocking collectives, per_device(): lax.psum(lax.psum((primal_local, dual_local), axis_name='blk'), axis_name...  17.7 us
    convert_element_type x8, other arithmetic, per_device(): weighted_share = (own_scale * (own_mult + aug_weight * (own_scale * prod_...  8.73 us
  transfers between devices with their start and end apart: 9, of which 8 were waited for; matrix products, arithmetic and copies ran while one was open for 1% of the time, Pallas kernels for 0%

profile of v1, /device:TPU:12, one launch (start us, length us, event | category | flops | bytes accessed | tf_op | source)
XLA Modules:
  0.0 345.2 jit_solution(7482902403306042536)
XLA Ops:
  7.3 4.6 %fusion.48 = f32[64,2048]{1,0:T(8,128)} fusion(bf16[2048,1024]{1,0:T(8,128)(2,1)} %param.10, f32[64,1024]{1,0:T(8,128)} %param.16), kind=kOutput, calls=%fused_computation.68 | convolution fusion | flops 268500992 | bytes 4980736 | tf_op jit(solution)/shard_map/dot_general | solution.py:29
  12.1 21.8 %reduce-scatter.10.cloned.1.call-done = f32[64,512]{1,0:T(8,128)} async-done(((f32[64,2048]{1,0:T(8,128)}), f32[64,512]{1,0:T(8,128)}) %reduce-scatter.10.cloned.1.call-update) | async-done | bytes 131088 | tf_op jit(solution)/shard_map/reduce_scatter | solution.py:32
  35.0 5.9 %all_gather.24 = bf16[64,2048]{1,0:T(8,128)(2,1)S(1)} all-gather(bf16[64,512]{1,0:T(8,128)(2,1)S(1)} %multiply_convert_fusion.7), channel_id=1, replica_groups=mesh['scen'=8,'blk'=4] {'blk'}, dimensions={1}, use_global_device_ids=true | all-gather | bytes 327680 | tf_op jit(solution)/shard_map/all_gather | solution.py:37
  40.9 3.1 fusion.17
  46.3 21.8 %reduce-scatter.12.cloned.1.call-done = f32[64,512]{1,0:T(8,128)} async-done(((f32[64,2048]{1,0:T(8,128)}), f32[64,512]{1,0:T(8,128)}) %reduce-scatter.12.cloned.1.call-update) | async-done | bytes 131088 | tf_op jit(solution)/shard_map/reduce_scatter | solution.py:32
  69.2 5.9 %all_gather.25 = bf16[64,2048]{1,0:T(8,128)(2,1)S(1)} all-gather(bf16[64,512]{1,0:T(8,128)(2,1)S(1)} %multiply_convert_fusion.6), channel_id=1, replica_groups=mesh['scen'=8,'blk'=4] {'blk'}, dimensions={1}, use_global_device_ids=true | all-gather | bytes 327680 | tf_op jit(solution)/shard_map/all_gather | solution.py:37
  75.1 3.1 fusion.19
  80.5 21.8 %reduce-scatter.14.cloned.1.call-done = f32[64,512]{1,0:T(8,128)} async-done(((f32[64,2048]{1,0:T(8,128)}), f32[64,512]{1,0:T(8,128)}) %reduce-scatter.14.cloned.1.call-update) | async-done | bytes 131088 | tf_op jit(solution)/shard_map/reduce_scatter | solution.py:32
  103.3 5.9 %all_gather.26 = bf16[64,2048]{1,0:T(8,128)(2,1)S(1)} all-gather(bf16[64,512]{1,0:T(8,128)(2,1)S(1)} %multiply_convert_fusion.5), channel_id=1, replica_groups=mesh['scen'=8,'blk'=4] {'blk'}, dimensions={1}, use_global_device_ids=true | all-gather | bytes 327680 | tf_op jit(solution)/shard_map/all_gather | solution.py:37
  109.2 3.1 fusion.21
  114.6 21.8 %reduce-scatter.16.cloned.1.call-done = f32[64,512]{1,0:T(8,128)} async-done(((f32[64,2048]{1,0:T(8,128)}), f32[64,512]{1,0:T(8,128)}) %reduce-scatter.16.cloned.1.call-update) | async-done | bytes 131088 | tf_op jit(solution)/shard_map/reduce_scatter | solution.py:32
  137.5 5.9 %all_gather.27 = bf16[64,2048]{1,0:T(8,128)(2,1)S(1)} all-gather(bf16[64,512]{1,0:T(8,128)(2,1)S(1)} %multiply_convert_fusion.4), channel_id=1, replica_groups=mesh['scen'=8,'blk'=4] {'blk'}, dimensions={1}, use_global_device_ids=true | all-gather | bytes 327680 | tf_op jit(solution)/shard_map/all_gather | solution.py:37
  148.8 21.8 %reduce-scatter.18.cloned.1.call-done = f32[64,512]{1,0:T(8,128)} async-done(((f32[64,2048]{1,0:T(8,128)}), f32[64,512]{1,0:T(8,128)}) %reduce-scatter.18.cloned.1.call-update) | async-done | bytes 131088 | tf_op jit(solution)/shard_map/reduce_scatter | solution.py:32
  171.6 5.9 %all_gather.28 = bf16[64,2048]{1,0:T(8,128)(2,1)S(1)} all-gather(bf16[64,512]{1,0:T(8,128)(2,1)S(1)} %multiply_convert_fusion.3), channel_id=1, replica_groups=mesh['scen'=8,'blk'=4] {'blk'}, dimensions={1}, use_global_device_ids=true | all-gather | bytes 327680 | tf_op jit(solution)/shard_map/all_gather | solution.py:37
  183.1 21.6 %reduce-scatter.20.cloned.1.call-done = f32[64,512]{1,0:T(8,128)} async-done(((f32[64,2048]{1,0:T(8,128)}), f32[64,512]{1,0:T(8,128)}) %reduce-scatter.20.cloned.1.call-update) | async-done | bytes 131088 | tf_op jit(solution)/shard_map/reduce_scatter | solution.py:32
  205.8 5.9 %all_gather.29 = bf16[64,2048]{1,0:T(8,128)(2,1)S(1)} all-gather(bf16[64,512]{1,0:T(8,128)(2,1)S(1)} %multiply_convert_fusion.2), channel_id=1, replica_groups=mesh['scen'=8,'blk'=4] {'blk'}, dimensions={1}, use_global_device_ids=true | all-gather | bytes 327680 | tf_op jit(solution)/shard_map/all_gather | solution.py:37
  217.1 21.8 %reduce-scatter.22.cloned.1.call-done = f32[64,512]{1,0:T(8,128)} async-done(((f32[64,2048]{1,0:T(8,128)}), f32[64,512]{1,0:T(8,128)}) %reduce-scatter.22.cloned.1.call-update) | async-done | bytes 131088 | tf_op jit(solution)/shard_map/reduce_scatter | solution.py:32
  239.9 5.9 %all_gather.30 = bf16[64,2048]{1,0:T(8,128)(2,1)S(1)} all-gather(bf16[64,512]{1,0:T(8,128)(2,1)S(1)} %multiply_convert_fusion.1), channel_id=1, replica_groups=mesh['scen'=8,'blk'=4] {'blk'}, dimensions={1}, use_global_device_ids=true | all-gather | bytes 327680 | tf_op jit(solution)/shard_map/all_gather | solution.py:37
  251.2 21.8 %reduce-scatter.24.cloned.1.call-done = f32[64,512]{1,0:T(8,128)} async-done(((f32[64,2048]{1,0:T(8,128)}), f32[64,512]{1,0:T(8,128)}) %reduce-scatter.24.cloned.1.call-update) | async-done | bytes 131088 | tf_op jit(solution)/shard_map/reduce_scatter | solution.py:32
  274.1 5.9 %all_gather.31 = bf16[64,2048]{1,0:T(8,128)(2,1)S(1)} all-gather(bf16[64,512]{1,0:T(8,128)(2,1)S(1)} %multiply_convert_fusion), channel_id=1, replica_groups=mesh['scen'=8,'blk'=4] {'blk'}, dimensions={1}, use_global_device_ids=true | all-gather | bytes 327680 | tf_op jit(solution)/shard_map/all_gather | solution.py:37
  280.0 3.1 multiply_reduce_fusion.1
  286.0 19.5 %all-reduce.1 = (f32[1024]{0:T(1024)S(1)}, f32[]{:T(128)}) all-reduce(f32[1024]{0:T(1024)S(1)} %get-tuple-element.16, f32[]{:T(128)} %reduce_sum.37), channel_id=1, replica_groups=mesh['scen'=8,'blk'=4] {'scen'}, use_global_device_ids=true, to_apply=%region_10.11 | all-reduce | flops 1025 | bytes 8200 | tf_op jit(solution)/shard_map/psum | solution.py:51
  308.7 6.3 %all-reduce.2 = (f32[]{:T(128)}, f32[]{:T(128)}) all-reduce(f32[]{:T(128)} %get-tuple-element.14, f32[]{:T(128)S(6)} %mul.128), channel_id=1, replica_groups=mesh['scen'=8,'blk'=4] {'blk'}, use_global_device_ids=true, to_apply=%region_14.15 | all-reduce | flops 2 | bytes 16 | tf_op jit(solution)/shard_map/psum | solution.py:56
  315.0 17.7 %all-reduce = (f32[]{:T(128)}, f32[]{:T(128)}) all-reduce(f32[]{:T(128)} %get-tuple-element.10, f32[]{:T(128)} %get-tuple-element.11), channel_id=1, replica_groups=mesh['scen'=8,'blk'=4] {'scen'}, use_global_device_ids=true, to_apply=%region_15.16 | all-reduce | flops 2 | bytes 16 | tf_op jit(solution)/shard_map/psum | solution.py:55
  (83 shorter events, 44.3 us)
Async XLA Ops:
  7.2 33.8 %copy-start.12 = (f32[64,1024]{1,0:T(8,128)S(1)}, f32[64,1024]{1,0:T(8,128)}, u32[]{:S(2)}) copy-start(f32[64,1024]{1,0:T(8,128)} %param.16) | copy-start | bytes 786436
  7.2 26.7 %copy-start.8 = (f32[64,2048]{1,0:T(8,128)S(1)}, f32[64,2048]{1,0:T(8,128)}, u32[]{:S(2)}) copy-start(f32[64,2048]{1,0:T(8,128)} %param.12) | copy-start | bytes 1572868
  7.2 26.7 %copy-start.9 = (f32[64,2048]{1,0:T(8,128)S(1)}, f32[64,2048]{1,0:T(8,128)}, u32[]{:S(2)}) copy-start(f32[64,2048]{1,0:T(8,128)} %param.13) | copy-start | bytes 1572868
  7.2 26.7 %copy-start.10 = (f32[64,2048]{1,0:T(8,128)S(1)}, f32[64,2048]{1,0:T(8,128)}, u32[]{:S(2)}) copy-start(f32[64,2048]{1,0:T(8,128)} %param.11) | copy-start | bytes 1572868
  7.2 33.7 %copy-start.15 = (f32[1024]{0:T(1024)S(1)}, f32[1024]{0:T(1024)}, u32[]{:S(2)}) copy-start(f32[1024]{0:T(1024)} %param.17) | copy-start | bytes 12292
  7.2 26.7 %reduce-scatter.10.cloned.1.call-start = ((), (), s32[]{:S(2)}) async-start(), calls=%async_computation.9 | async-start | bytes 655360 | tf_op jit(solution)/shard_map/reduce_scatter | solution.py:32
  11.9 56.2 %reduce-scatter.12.cloned.1.call-start = ((), (), s32[]{:S(2)}) async-start(), calls=%async_computation.10 | async-start | bytes 655360 | tf_op jit(solution)/shard_map/reduce_scatter | solution.py:32
  33.9 10.1 %copy-start = (bf16[2048,1024]{1,0:T(8,128)(2,1)S(1)}, bf16[2048,1024]{1,0:T(8,128)(2,1)}, u32[]{:S(2)}) copy-start(bf16[2048,1024]{1,0:T(8,128)(2,1)} %param.10) | copy-start | bytes 12582916
  46.3 56.0 %reduce-scatter.14.cloned.1.call-start = ((), (), s32[]{:S(2)}) async-start(), calls=%async_computation.11 | async-start | bytes 655360 | tf_op jit(solution)/shard_map/reduce_scatter | solution.py:32
  68.1 10.1 %copy-start.1 = (bf16[2048,1024]{1,0:T(8,128)(2,1)S(1)}, bf16[2048,1024]{1,0:T(8,128)(2,1)}, u32[]{:S(2)}) copy-start(bf16[2048,1024]{1,0:T(8,128)(2,1)} %param.10) | copy-start | bytes 12582916
  80.4 56.0 %reduce-scatter.16.cloned.1.call-start = ((), (), s32[]{:S(2)}) async-start(), calls=%async_computation.12 | async-start | bytes 655360 | tf_op jit(solution)/shard_map/reduce_scatter | solution.py:32
  102.2 10.1 %copy-start.2 = (bf16[2048,1024]{1,0:T(8,128)(2,1)S(1)}, bf16[2048,1024]{1,0:T(8,128)(2,1)}, u32[]{:S(2)}) copy-start(bf16[2048,1024]{1,0:T(8,128)(2,1)} %param.10) | copy-start | bytes 12582916
  114.6 56.0 %reduce-scatter.18.cloned.1.call-start = ((), (), s32[]{:S(2)}) async-start(), calls=%async_computation.13 | async-start | bytes 655360 | tf_op jit(solution)/shard_map/reduce_scatter | solution.py:32
  136.4 10.1 %copy-start.3 = (bf16[2048,1024]{1,0:T(8,128)(2,1)S(1)}, bf16[2048,1024]{1,0:T(8,128)(2,1)}, u32[]{:S(2)}) copy-start(bf16[2048,1024]{1,0:T(8,128)(2,1)} %param.10) | copy-start | bytes 12582916
  148.7 56.0 %reduce-scatter.20.cloned.1.call-start = ((), (), s32[]{:S(2)}) async-start(), calls=%async_computation.14 | async-start | bytes 655360 | tf_op jit(solution)/shard_map/reduce_scatter | solution.py:32
  170.5 10.1 %copy-start.4 = (bf16[2048,1024]{1,0:T(8,128)(2,1)S(1)}, bf16[2048,1024]{1,0:T(8,128)(2,1)}, u32[]{:S(2)}) copy-start(bf16[2048,1024]{1,0:T(8,128)(2,1)} %param.10) | copy-start | bytes 12582916
  182.9 56.0 %reduce-scatter.22.cloned.1.call-start = ((), (), s32[]{:S(2)}) async-start(), calls=%async_computation.15 | async-start | bytes 655360 | tf_op jit(solution)/shard_map/reduce_scatter | solution.py:32
  217.0 56.0 %reduce-scatter.24.cloned.1.call-start = ((), (), s32[]{:S(2)}) async-start(), calls=%async_computation.16 | async-start | bytes 655360 | tf_op jit(solution)/shard_map/reduce_scatter | solution.py:32
  238.8 10.1 %copy-start.6 = (bf16[2048,1024]{1,0:T(8,128)(2,1)S(1)}, bf16[2048,1024]{1,0:T(8,128)(2,1)}, u32[]{:S(2)}) copy-start(bf16[2048,1024]{1,0:T(8,128)(2,1)} %param.10) | copy-start | bytes 12582916
  248.9 31.1 %copy-start.18 = (f32[64]{0:T(128)S(1)}, f32[64]{0:T(128)}, u32[]{:S(2)}) copy-start(f32[64]{0:T(128)} %param.19) | copy-start | bytes 772
  251.2 83.6 %reduce-scatter.26.cloned.1.call-start = ((), (), s32[]{:S(2)}) async-start(), calls=%async_computation.17 | async-start | bytes 655360 | tf_op jit(solution)/shard_map/reduce_scatter | solution.py:46
  273.0 10.1 %copy-start.7 = (bf16[2048,1024]{1,0:T(8,128)(2,1)S(1)}, bf16[2048,1024]{1,0:T(8,128)(2,1)}, u32[]{:S(2)}) copy-start(bf16[2048,1024]{1,0:T(8,128)(2,1)} %param.10) | copy-start | bytes 12582916
  283.1 53.3 %copy-start.11 = (f32[64,1024]{1,0:T(8,128)}, f32[64,1024]{1,0:T(8,128)S(1)}, u32[]{:S(2)}) copy-start(f32[64,1024]{1,0:T(8,128)S(1)} %get-tuple-element.17) | copy-start | bytes 786436
  306.7 29.7 %copy-start.17 = (f32[1024]{0:T(1024)}, f32[1024]{0:T(1024)S(1)}, u32[]{:S(2)}) copy-start(f32[1024]{0:T(1024)S(1)} %get-tuple-element.13) | copy-start | bytes 12292
  (4 other events, 24.5 us)
Sparse Core Ops, SparseCore 0:
  12.0 21.8 reduce-scatter.9
  46.4 21.6 reduce-scatter.11
  80.5 21.6 reduce-scatter.13
  114.7 21.6 reduce-scatter.15
  148.8 21.6 reduce-scatter.17
  183.0 21.6 reduce-scatter.19
  217.1 21.6 reduce-scatter.21
  251.3 21.6 reduce-scatter.23
  285.5 21.6 reduce-scatter.25
